TPU v7x, 32 devices: a whole 2x2x4 slice. The times are simulated.
32 devices in a mesh: groups: 2 (over y), plane: 4 (over z), depth: 2 (over x), tok: 2 (over core).
Axes of the slice: x: 2, y: 2, z: 4, core: 2. Of those that a mesh axis runs over, the one named last changes fastest.
Arguments:
- tokens: bfloat16 [256, 2048], P(('groups', 'plane', 'depth', 'tok')), parts along dimension 0, may hold values from -6 to 6
- expert_ids: int32 [256, 4], P(('groups', 'plane', 'depth', 'tok')), parts along dimension 0, may hold values from 0 to 3, as said below
- slot_index: int32 [256, 4], P(('groups', 'plane', 'depth', 'tok')), parts along dimension 0, may hold values from 0 to 7, as said below
- route_weight: bfloat16 [256, 4], P(('groups', 'plane', 'depth', 'tok')), parts along dimension 0, may hold values from 0.099609375 to 1
- shared_gate: bfloat16 [2048], replicated, may hold values from -0.125 to 0.125
- shared_gate_up: bfloat16 [2, 2048, 5632], P(None, None, 'plane'), may hold values from -0.125 to 0.125
- shared_down: bfloat16 [5632, 2048], P('plane'), may hold values from -0.078125 to 0.078125
- expert_gate_up: bfloat16 [4, 2, 2048, 1408], P('plane', None, None, ('depth', 'tok')), may hold values from -0.125 to 0.125
- expert_down: bfloat16 [4, 1408, 2048], P('plane', ('depth', 'tok')), may hold values from -0.15625 to 0.15625
Outputs:
- mixed: bfloat16 [256, 2048], P(('groups', 'plane', 'depth', 'tok')), parts along dimension 0
There are 2 independent parts, one for each index of `groups`. A program takes and returns all parts, laid end to end along the dimension named above; an argument that names none is the same for every part. Nothing has to cross between parts.
Inputs may be any that keep to these rules, and one draw needn't show every extreme that they name: `expert_ids`: each row names 4 different experts. Among the choices of the rows of one device that name the same expert, slot_index takes each value from 0 to their count minus one exactly once, in an order that varies from draw to draw; the capacity 8 is filled on some devices.
All inputs are finite; a program needn't handle non-finite values.
Results may differ from a plain program's by a relative error of at most 0.019.
Values may be sent and summed in bfloat16 or wider, within the bound.
A program may use at most 64 MiB of HBM per device.

v0:
```python
import jax
import jax.numpy as jnp
from jax import lax
from jax.sharding import PartitionSpec as P


def gated_rows(token_rows, gate_up):
    gate_part = jnp.dot(token_rows, gate_up[0], preferred_element_type=jnp.float32)
    up_part = jnp.dot(token_rows, gate_up[1], preferred_element_type=jnp.float32)
    return (jax.nn.silu(gate_part) * up_part).astype(jnp.bfloat16)


def expert_rows(received, gate_up, down_proj):
    hidden = gated_rows(lax.all_gather(received, ("depth", "tok"), axis=0, tiled=True), gate_up)
    return lax.psum_scatter(
        jnp.dot(hidden, down_proj, preferred_element_type=jnp.float32).astype(jnp.bfloat16),
        ("depth", "tok"),
        scatter_dimension=0,
        tiled=True,
    ).astype(jnp.float32)


def on_device(
    tokens,
    expert_ids,
    slot_index,
    route_weight,
    shared_gate,
    shared_gate_up,
    shared_down,
    expert_gate_up,
    expert_down,
):
    planes = lax.axis_size("plane")
    tok_rows = tokens.shape[0]
    choose_count = expert_ids.shape[1]
    model_width = tokens.shape[1]
    capacity = max(2, tok_rows * choose_count // planes)
    slot_total = planes * capacity
    local_gate_up = expert_gate_up[0]
    local_down = expert_down[0]
    column = lax.broadcasted_iota(jnp.int32, (slot_total, 1, 1), 0)
    kept_mask = slot_index < capacity
    target = jnp.where(kept_mask, expert_ids * capacity + slot_index, -1)
    matches = target[None, :, :] == column
    spread = jnp.any(matches, axis=2).astype(jnp.bfloat16)
    outgoing = jnp.dot(spread, tokens, preferred_element_type=jnp.float32).astype(jnp.bfloat16)
    outgoing = outgoing.reshape(planes, capacity, model_width)
    routed_slots = lax.all_to_all(
        expert_rows(
            lax.all_to_all(outgoing, "plane", split_axis=0, concat_axis=0, tiled=True),
            local_gate_up,
            local_down,
        ).astype(jnp.bfloat16),
        "plane",
        split_axis=0,
        concat_axis=0,
        tiled=True,
    ).astype(jnp.float32)
    weights = route_weight.astype(jnp.float32)
    combine = jnp.sum(jnp.where(matches, weights[None, :, :], 0.0), axis=2).T
    routed = jnp.dot(
        combine,
        routed_slots.reshape(slot_total, model_width),
        precision=lax.Precision.HIGHEST,
        preferred_element_type=jnp.float32,
    )
    shared_hidden = gated_rows(lax.all_gather(tokens, "plane", axis=0, tiled=True), shared_gate_up)
    shared_out = lax.psum_scatter(
        jnp.dot(shared_hidden, shared_down, preferred_element_type=jnp.float32).astype(
            jnp.bfloat16
        ),
        "plane",
        scatter_dimension=0,
        tiled=True,
    ).astype(jnp.float32)
    shared_scale = jax.nn.sigmoid(jnp.dot(tokens, shared_gate, preferred_element_type=jnp.float32))
    result = shared_scale[:, None] * shared_out + routed
    return result.astype(jnp.bfloat16)


def solution(mesh):
    in_specs = (
        P(("groups", "plane", "depth", "tok"), None),
        P(("groups", "plane", "depth", "tok"), None),
        P(("groups", "plane", "depth", "tok"), None),
        P(("groups", "plane", "depth", "tok"), None),
        P(),
        P(None, None, "plane"),
        P("plane", None),
        P("plane", None, None, ("depth", "tok")),
        P("plane", ("depth", "tok"), None),
    )
    out_specs = P(("groups", "plane", "depth", "tok"), None)
    return jax.shard_map(
        on_device, mesh=mesh, in_specs=in_specs, out_specs=out_specs, check_vma=False
    )
```

profile of v0, /device:TPU:0, one launch (start us, length us, event | category | flops | bytes accessed | tf_op | source)
XLA Modules:
  0.0 94.5 jit_solution(18416283824460108339)
XLA Ops:
  6.5 0.8 add_select_fusion
  7.4 0.1 fusion.48
  7.4 1.6 %fusion.12 = bf16[4,8,2048]{2,1,0:T(8,128)(2,1)} fusion(pred[32,8]{0,1:T(8,128)(4,1)S(1)} %fusion.48, bf16[8,2048]{1,0:T(8,128)(2,1)} %param.9), kind=kOutput, calls=%fused_computation.11 | convolution fusion | flops 1114112 | bytes 164096 | tf_op jit(solution)/shard_map/dot_general | solution.py:47
  9.1 6.3 %all-to-all-start = ((bf16[4,8,2048]{2,1,0:T(8,128)(2,1)}), bf16[4,8,2048]{2,1,0:T(8,128)(2,1)S(1)}, u32[]{:S(2)}, u32[]{:S(2)}) async-start(bf16[4,8,2048]{2,1,0:T(8,128)(2,1)} %fusion.12), calls=%async_computation.1 | async-start | bytes 262144 | tf_op jit(solution)/shard_map/all_to_all | solution.py:51
  15.4 14.1 %all_gather.6 = bf16[32,2048]{1,0:T(8,128)(2,1)S(1)} all-gather(bf16[8,2048]{1,0:T(8,128)(2,1)} %param.9), channel_id=1, replica_groups=mesh['groups'=2,'plane'=4,'depth'=2,'tok'=2] {'plane'}, dimensions={0}, use_global_device_ids=true | all-gather | bytes 163840 | tf_op jit(solution)/shard_map/all_gather | solution.py:68
  29.6 0.0 all-to-all-done
  29.6 7.2 %all_gather.7 = bf16[16,8,2048]{2,1,0:T(8,128)(2,1)S(1)} all-gather(bf16[4,8,2048]{2,1,0:T(8,128)(2,1)S(1)} %all-to-all-done), channel_id=1, replica_groups=mesh['groups'=2,'plane'=4,'depth'=2,'tok'=2] {'depth','tok'}, dimensions={0}, use_global_device_ids=true | all-gather | bytes 655360 | tf_op jit(solution)/shard_map/all_gather | solution.py:14
  36.7 2.0 %fusion.16 = f32[16,8,352]{2,1,0:T(8,128)S(1)} fusion(bf16[16,8,2048]{2,1,0:T(8,128)(2,1)S(1)} %all_gather.7, bf16[1,2,2048,352]{2,3,1,0:T(8,128)(2,1)} %param.16), kind=kOutput, calls=%fused_computation.16 | convolution fusion | flops 184549376 | bytes 2146304 | tf_op jit(solution)/shard_map/dot_general | solution.py:8
  38.7 3.4 %convolution_convert_fusion = bf16[16,8,2048]{2,1,0:T(8,128)(2,1)} fusion(bf16[1,352,2048]{2,1,0:T(8,128)(2,1)S(1)} %copy-done, bf16[16,8,2048]{2,1,0:T(8,128)(2,1)S(1)} %all_gather.7, bf16[1,2,2048,352]{2,3,1,0:T(8,128)(2,1)} %param.16, f32[16,8,352]{2,1,0:T(8,128)S(1)} %fusion.16), kind=kOutput, calls=%fused_computation.6 | convolution fusion | flops 369631232 | bytes 4112384 | tf_op jit(solution)/shard_map/dot_general | solution.py:16
  42.1 0.0 reduce-scatter.5.cloned.1.call-update
  42.1 0.0 reduce-scatter.3.cloned.1.call-start
  42.2 3.7 %fusion.2 = f32[32,1408]{1,0:T(8,128)S(1)} fusion(bf16[32,2048]{1,0:T(8,128)(2,1)S(1)} %all_gather.6, bf16[2,2048,1408]{2,1,0:T(8,128)(2,1)} %param.14), kind=kOutput, calls=%fused_computation.2 | convolution fusion | flops 184549376 | bytes 6078464 | tf_op jit(solution)/shard_map/dot_general | solution.py:8
  45.8 0.0 copy-start.3
  45.8 0.0 copy-start.2
  45.9 0.0 copy-start.1
  45.9 7.2 %convolution_convert_fusion.2 = bf16[32,2048]{1,0:T(8,128)(2,1)} fusion(bf16[1408,2048]{1,0:T(8,128)(2,1)} %param.15, bf16[32,2048]{1,0:T(8,128)(2,1)S(1)} %all_gather.6, bf16[2,2048,1408]{2,1,0:T(8,128)(2,1)} %param.14, f32[32,1408]{1,0:T(8,128)S(1)} %fusion.2), kind=kOutput, calls=%fused_computation.10 | convolution fusion | flops 369434624 | bytes 11976704 | tf_op jit(solution)/shard_map/dot_general | solution.py:70
  53.1 0.0 reduce-scatter.3.cloned.1.call-update
  53.1 0.1 select_reduce_fusion
  53.2 11.1 %reduce-scatter.5.cloned.1.call-done = bf16[4,8,2048]{2,1,0:T(8,128)(2,1)} async-done(((bf16[16,8,2048]{2,1,0:T(8,128)(2,1)}), bf16[4,8,2048]{2,1,0:T(8,128)(2,1)}) %reduce-scatter.5.cloned.1.call-update) | async-done | bytes 131088 | tf_op jit(solution)/shard_map/reduce_scatter | solution.py:15
  64.3 4.6 %all-to-all-start.1 = ((bf16[4,8,2048]{2,1,0:T(8,128)(2,1)}), bf16[4,8,2048]{2,1,0:T(8,128)(2,1)S(1)}, u32[]{:S(2)}, u32[]{:S(2)}) async-start(bf16[4,8,2048]{2,1,0:T(8,128)(2,1)} %reduce-scatter.5.cloned.1.call-done), calls=%async_computation.3 | async-start | bytes 262144 | tf_op jit(solution)/shard_map/all_to_all | solution.py:49
  69.0 0.1 fusion.32
  69.1 17.0 %reduce-scatter.3.cloned.1.call-done = bf16[8,2048]{1,0:T(8,128)(2,1)} async-done(((bf16[32,2048]{1,0:T(8,128)(2,1)}), bf16[8,2048]{1,0:T(8,128)(2,1)}) %reduce-scatter.3.cloned.1.call-update) | async-done | bytes 32784 | tf_op jit(solution)/shard_map/reduce_scatter | solution.py:69
  86.1 0.0 all-to-all-done.1
  86.1 1.5 %fusion.13 = bf16[8,2048]{1,0:T(8,128)(2,1)} fusion(f32[32,8]{0,1:T(8,128)S(1)} %select_reduce_fusion, bf16[4,8,2048]{2,1,0:T(8,128)(2,1)S(1)} %all-to-all-done.1, bf16[8,2048]{1,0:T(8,128)(2,1)} %reduce-scatter.3.cloned.1.call-done, f32[8]{0:T(128)S(1)} %fusion.32), kind=kOutput, calls=%fused_computation.13 | convolution fusion | flops 6356992 | bytes 197664 | tf_op jit(solution)/shard_map/dot_general | solution.py:62
  (8 shorter events, 0.0 us)
Async XLA Ops:
  6.5 32.2 %copy-start = (bf16[1,352,2048]{2,1,0:T(8,128)(2,1)S(1)}, bf16[1,352,2048]{2,1,0:T(8,128)(2,1)}, u32[]{:S(2)}) copy-start(bf16[1,352,2048]{2,1,0:T(8,128)(2,1)} %param.17) | copy-start | bytes 4325380
  9.1 20.5 %all-to-all-start = ((bf16[4,8,2048]{2,1,0:T(8,128)(2,1)}), bf16[4,8,2048]{2,1,0:T(8,128)(2,1)S(1)}, u32[]{:S(2)}, u32[]{:S(2)}) async-start(bf16[4,8,2048]{2,1,0:T(8,128)(2,1)} %fusion.12), calls=%async_computation.1 | async-start | bytes 262144 | tf_op jit(solution)/shard_map/all_to_all | solution.py:51
  15.4 48.9 %reduce-scatter.5.cloned.1.call-start = ((), (), s32[]{:S(2)}) async-start(), calls=%async_computation.5 | async-start | bytes 655360 | tf_op jit(solution)/shard_map/reduce_scatter | solution.py:15
  42.1 44.0 %reduce-scatter.3.cloned.1.call-start = ((), (), s32[]{:S(2)}) async-start(), calls=%async_computation.4 | async-start | bytes 163840 | tf_op jit(solution)/shard_map/reduce_scatter | solution.py:69
  45.8 7.3 %copy-start.3 = (bf16[8,4]{0,1:T(4,128)(2,1)S(1)}, bf16[8,4]{0,1:T(4,128)(2,1)}, u32[]{:S(2)}) copy-start(bf16[8,4]{0,1:T(4,128)(2,1)} %param.12) | copy-start | bytes 196
  45.8 7.4 %copy-start.2 = (bf16[2048]{0:T(1024)(128)(2,1)S(1)}, bf16[2048]{0:T(1024)(128)(2,1)}, u32[]{:S(2)}) copy-start(bf16[2048]{0:T(1024)(128)(2,1)} %param.13) | copy-start | bytes 12292
  45.9 23.1 %copy-start.1 = (bf16[8,2048]{1,0:T(8,128)(2,1)S(1)}, bf16[8,2048]{1,0:T(8,128)(2,1)}, u32[]{:S(2)}) copy-start(bf16[8,2048]{1,0:T(8,128)(2,1)} %param.9) | copy-start | bytes 98308
  64.3 21.7 %all-to-all-start.1 = ((bf16[4,8,2048]{2,1,0:T(8,128)(2,1)}), bf16[4,8,2048]{2,1,0:T(8,128)(2,1)S(1)}, u32[]{:S(2)}, u32[]{:S(2)}) async-start(bf16[4,8,2048]{2,1,0:T(8,128)(2,1)} %reduce-scatter.5.cloned.1.call-done), calls=%async_computation.3 | async-start | bytes 262144 | tf_op jit(solution)/shard_map/all_to_all | solution.py:49
Sparse Core Ops, SparseCore 0:
  42.2 22.0 reduce-scatter.4
  66.6 19.4 reduce-scatter.2
where the time goes:
time: 95 us; the launch traced here: 94.5 us
  waiting for transfers between devices  28.1 us (30%)
  blocking collectives  21.3 us (22%)
  matrix products  19.5 us (21%)
  between operations  13.5 us (14%)
  starting transfers between devices  11 us (12%)
  other arithmetic  0.97 us (1%)
    reduce_scatter x1, waiting for transfers between devices, on_device(): lax.psum_scatter(jnp.dot(shared_hidden, shared_down, preferred_element_ty...  17 us
    all_gather x1, blocking collectives, on_device(): lax.all_gather(tokens, 'plane', axis=0, tiled=True)  14.1 us
    reduce_scatter x1, waiting for transfers between devices, expert_rows(): lax.psum_scatter(jnp.dot(hidden, down_proj, preferred_element_type=jnp.fl...  11.1 us
    dot_general x1, matrix products, on_device(): jnp.dot(shared_hidden, shared_down, preferred_element_type=jnp.float32)  7.22 us
    all_gather x1, blocking collectives, expert_rows(): lax.all_gather(received, ('depth', 'tok'), axis=0, tiled=True)  7.16 us
    all_to_all x1, starting transfers between devices, on_device(): lax.all_to_all(outgoing, 'plane', split_axis=0, concat_axis=0, tiled=True)  6.35 us
    dot_general x2, matrix products, gated_rows(): jnp.dot(token_rows, gate_up[0], preferred_element_type=jnp.float32)  5.62 us
    all_to_all x1, starting transfers between devices, on_device(): lax.all_to_all(expert_rows(lax.all_to_all(outgoing, 'plane', split_axis=0...  4.6 us
  transfers between devices with their start and end apart: 4, of which 2 were waited for; matrix products, arithmetic and copies ran while one was open for 12% of the time, Pallas kernels for 0%

commit v1 on v0

--- a/solution.py
+++ b/solution.py
@@ -2,6 +2,18 @@
 import jax.numpy as jnp
 from jax import lax
 from jax.sharding import PartitionSpec as P
+
+
+def doubled_up(x, axis, dim):
+    ways, here = (lax.axis_size(axis), lax.axis_index(axis))
+    grown, reach = (x, 1)
+    while reach < ways:
+        theirs = lax.ppermute(grown, axis, [(d, d ^ reach) for d in range(ways)])
+        mine_first = jnp.concatenate([grown, theirs], axis=dim)
+        theirs_first = jnp.concatenate([theirs, grown], axis=dim)
+        grown = jnp.where(here & reach == 0, mine_first, theirs_first)
+        reach = 2 * reach
+    return grown
 
 
 def gated_rows(token_rows, gate_up):
@@ -11,7 +23,7 @@
 
 
 def expert_rows(received, gate_up, down_proj):
-    hidden = gated_rows(lax.all_gather(received, ("depth", "tok"), axis=0, tiled=True), gate_up)
+    hidden = gated_rows(doubled_up(received, ("depth", "tok"), 0), gate_up)
     return lax.psum_scatter(
         jnp.dot(hidden, down_proj, preferred_element_type=jnp.float32).astype(jnp.bfloat16),
         ("depth", "tok"),

time: 95 us -> 93.2 us (0.981)
  starting transfers between devices: 11 us -> 6.21 us
  blocking collectives: 21.3 us -> 25.9 us
    all_to_all x0 -> x1, blocking collectives: none -> 12.2 us  [on_device(): lax.all_to_all(outgoing, 'plane', split_axis=0, concat_axis=0, tiled=True)]
    all_gather x1 -> x0, blocking collectives: 7.16 us -> none  [expert_rows(): lax.all_gather(received, ('depth', 'tok'), axis=0, tiled=True)]
    all_to_all x1 -> x0, starting transfers between devices: 6.35 us -> none  [on_device(): lax.all_to_all(outgoing, 'plane', split_axis=0, concat_axis=0, tiled=True)]
    reduce_scatter x1, waiting for transfers between devices: 11.1 us -> 8.87 us  [expert_rows(): lax.psum_scatter(jnp.dot(hidden, down_proj, preferred_element_type=jnp.fl...]
    dot_general x0 -> x1, matrix products: none -> 1.97 us  [gated_rows(): jnp.dot(token_rows, gate_up[1], preferred_element_type=jnp.float32)]
    dot_general x2 -> x1, matrix products: 5.62 us -> 3.66 us  [gated_rows(): jnp.dot(token_rows, gate_up[0], preferred_element_type=jnp.float32)]
    ppermute x0 -> x2, starting transfers between devices: none -> 1.56 us  [doubled_up(): theirs = lax.ppermute(grown, axis, [(d, d ^ reach) for d in range(ways)])]
    ppermute x0 -> x2, waiting for transfers between devices: none -> 1.35 us  [doubled_up(): theirs = lax.ppermute(grown, axis, [(d, d ^ reach) for d in range(ways)])]
  transfers between devices with their start and end apart: 4 -> 5, of which waited for: 2 -> 3; matrix products, arithmetic and copies ran while one was open for 12% -> 12% of each run, Pallas kernels for 0% -> 0%
where the time goes in v1:
time: 93.2 us; the launch traced here: 92.8 us
  waiting for transfers between devices  27.2 us (29%)
  blocking collectives  25.9 us (28%)
  matrix products  18.9 us (20%)
  between operations  13.5 us (14%)
  starting transfers between devices  6.21 us (7%)
  other arithmetic  1 us (1%)
    reduce_scatter x1, waiting for transfers between devices, on_device(): lax.psum_scatter(jnp.dot(shared_hidden, shared_down, preferred_element_ty...  17 us
    all_gather x1, blocking collectives, on_device(): lax.all_gather(tokens, 'plane', axis=0, tiled=True)  13.7 us
    all_to_all x1, blocking collectives, on_device(): lax.all_to_all(outgoing, 'plane', split_axis=0, concat_axis=0, tiled=True)  12.2 us
    reduce_scatter x1, waiting for transfers between devices, expert_rows(): lax.psum_scatter(jnp.dot(hidden, down_proj, preferred_element_type=jnp.fl...  8.87 us
    dot_general x1, matrix products, on_device(): jnp.dot(shared_hidden, shared_down, preferred_element_type=jnp.float32)  7.23 us
    all_to_all x1, starting transfers between devices, on_device(): lax.all_to_all(expert_rows(lax.all_to_all(outgoing, 'plane', split_axis=0...  4.6 us
    dot_general x1, matrix products, gated_rows(): jnp.dot(token_rows, gate_up[0], preferred_element_type=jnp.float32)  3.66 us
    dot_general x1, matrix products, expert_rows(): jnp.dot(hidden, down_proj, preferred_element_type=jnp.float32)  3.4 us
  transfers between devices with their start and end apart: 5, of which 3 were waited for; matrix products, arithmetic and copies ran while one was open for 12% of the time, Pallas kernels for 0%

profile of v1, /device:TPU:0, one launch (start us, length us, event | category | flops | bytes accessed | tf_op | source)
XLA Modules:
  0.0 92.8 jit_solution(9442800633254162574)
XLA Ops:
  6.5 0.8 add_select_fusion
  7.4 0.1 fusion.39
  7.4 1.0 %fusion.12 = bf16[4,8,2048]{2,1,0:T(8,128)(2,1)S(1)} fusion(pred[32,8]{0,1:T(8,128)(4,1)S(1)} %fusion.39, bf16[8,2048]{1,0:T(8,128)(2,1)} %param.9), kind=kOutput, calls=%fused_computation.11 | convolution fusion | flops 1114112 | bytes 164096 | tf_op jit(solution)/shard_map/dot_general | solution.py:59
  8.4 12.2 %all_to_all.10 = bf16[4,8,2048]{2,1,0:T(8,128)(2,1)S(1)} all-to-all(bf16[4,8,2048]{2,1,0:T(8,128)(2,1)S(1)} %fusion.12), channel_id=1, replica_groups=mesh['groups'=2,'plane'=4,'depth'=2,'tok'=2] {'plane'}, dimensions={0} | all-to-all | bytes 262144 | tf_op jit(solution)/shard_map/all_to_all | solution.py:63
  20.6 0.0 collective-permute-start
  20.6 1.3 %collective-permute-done = bf16[4,8,2048]{2,1,0:T(8,128)(2,1)S(1)} collective-permute-done((bf16[4,8,2048]{2,1,0:T(8,128)(2,1)S(1)}, bf16[4,8,2048]{2,1,0:T(8,128)(2,1)S(1)}, u32[]{:S(2)}, u32[]{:S(2)}) %collective-permute-start) | collective-permute-done | bytes 131104 | tf_op jit(solution)/shard_map/ppermute | solution.py:11
  22.0 1.6 %collective-permute-start.1 = (bf16[8,8,2048]{2,1,0:T(8,128)(2,1)S(1)}, bf16[8,8,2048]{2,1,0:T(8,128)(2,1)S(1)}, u32[]{:S(2)}, u32[]{:S(2)}) collective-permute-start(bf16[8,8,2048]{2,1,0:T(8,128)(2,1)S(1)} %maximum_select_fusion.1), channel_id=1, source_target_pairs={{0,2},{1,3},{2,0},{3,1},{4,6},{5,7},{6,4},{7,5},{8,10},{9,11},{10,... | collective-permute-start | bytes 786440 | tf_op jit(solution)/shard_map/ppermute | solution.py:11
  23.6 13.7 %all_gather.3 = bf16[32,2048]{1,0:T(8,128)(2,1)S(1)} all-gather(bf16[8,2048]{1,0:T(8,128)(2,1)} %param.9), channel_id=1, replica_groups=mesh['groups'=2,'plane'=4,'depth'=2,'tok'=2] {'plane'}, dimensions={0}, use_global_device_ids=true | all-gather | bytes 163840 | tf_op jit(solution)/shard_map/all_gather | solution.py:80
  37.2 2.0 %fusion.14 = f32[16,8,352]{2,1,0:T(8,128)S(1)} fusion(bf16[1,2,2048,352]{2,3,1,0:T(8,128)(2,1)} %param.16, bf16[8,8,2048]{2,1,0:T(8,128)(2,1)S(1)} %collective-permute-done.1, bf16[8,8,2048]{2,1,0:T(8,128)(2,1)S(1)} %maximum_select_fusion.1, pred[]{:T(512)S(6)} %eq.22), kind=kOutput, calls=%fused_computation.14 | convolution fusion | flops 185335808 | bytes 2146305 | tf_op jit(solution)/shard_map/dot_general | solution.py:21
  39.2 3.4 %convolution_convert_fusion = bf16[16,8,2048]{2,1,0:T(8,128)(2,1)} fusion(bf16[1,352,2048]{2,1,0:T(8,128)(2,1)S(1)} %copy-done, f32[16,8,352]{2,1,0:T(8,128)S(1)} %fusion.14, bf16[1,2,2048,352]{2,3,1,0:T(8,128)(2,1)} %param.16, bf16[8,8,2048]{2,1,0:T(8,128)(2,1)S(1)} %collective-permute-done.1, bf16[8,8,2048]{2,1,0:T(8,128)(2,1)S(1)} %maximum_select_fusion.1, ...), kind=kOutput, calls=%fused_computation.6 | convolution fusion | flops 370417664 | bytes 4112385 | tf_op jit(solution)/shard_map/dot_general | solution.py:28
  42.6 0.0 reduce-scatter.5.cloned.1.call-update
  42.6 0.0 reduce-scatter.3.cloned.1.call-start
  42.7 3.7 %fusion.2 = f32[32,1408]{1,0:T(8,128)S(1)} fusion(bf16[32,2048]{1,0:T(8,128)(2,1)S(1)} %all_gather.3, bf16[2,2048,1408]{2,1,0:T(8,128)(2,1)} %param.14), kind=kOutput, calls=%fused_computation.2 | convolution fusion | flops 184549376 | bytes 6078464 | tf_op jit(solution)/shard_map/dot_general | solution.py:20
  46.4 0.0 copy-start.3
  46.4 0.0 copy-start.2
  46.4 0.0 copy-start.1
  46.4 7.2 %convolution_convert_fusion.2 = bf16[32,2048]{1,0:T(8,128)(2,1)} fusion(bf16[1408,2048]{1,0:T(8,128)(2,1)} %param.15, bf16[32,2048]{1,0:T(8,128)(2,1)S(1)} %all_gather.3, bf16[2,2048,1408]{2,1,0:T(8,128)(2,1)} %param.14, f32[32,1408]{1,0:T(8,128)S(1)} %fusion.2), kind=kOutput, calls=%fused_computation.10 | convolution fusion | flops 369434624 | bytes 11976704 | tf_op jit(solution)/shard_map/dot_general | solution.py:82
  53.6 0.0 reduce-scatter.3.cloned.1.call-update
  53.7 0.1 select_reduce_fusion
  53.8 8.9 %reduce-scatter.5.cloned.1.call-done = bf16[4,8,2048]{2,1,0:T(8,128)(2,1)} async-done(((bf16[16,8,2048]{2,1,0:T(8,128)(2,1)}), bf16[4,8,2048]{2,1,0:T(8,128)(2,1)}) %reduce-scatter.5.cloned.1.call-update) | async-done | bytes 131088 | tf_op jit(solution)/shard_map/reduce_scatter | solution.py:27
  62.6 4.6 %all-to-all-start.1 = ((bf16[4,8,2048]{2,1,0:T(8,128)(2,1)}), bf16[4,8,2048]{2,1,0:T(8,128)(2,1)S(1)}, u32[]{:S(2)}, u32[]{:S(2)}) async-start(bf16[4,8,2048]{2,1,0:T(8,128)(2,1)} %reduce-scatter.5.cloned.1.call-done), calls=%async_computation.3 | async-start | bytes 262144 | tf_op jit(solution)/shard_map/all_to_all | solution.py:61
  67.2 0.1 fusion.24
  67.4 17.0 %reduce-scatter.3.cloned.1.call-done = bf16[8,2048]{1,0:T(8,128)(2,1)} async-done(((bf16[32,2048]{1,0:T(8,128)(2,1)}), bf16[8,2048]{1,0:T(8,128)(2,1)}) %reduce-scatter.3.cloned.1.call-update) | async-done | bytes 32784 | tf_op jit(solution)/shard_map/reduce_scatter | solution.py:81
  84.4 1.5 %fusion.13 = bf16[8,2048]{1,0:T(8,128)(2,1)} fusion(f32[32,8]{0,1:T(8,128)S(1)} %select_reduce_fusion, bf16[4,8,2048]{2,1,0:T(8,128)(2,1)S(1)} %all-to-all-done.1, bf16[8,2048]{1,0:T(8,128)(2,1)} %reduce-scatter.3.cloned.1.call-done, f32[8]{0:T(128)S(1)} %fusion.24), kind=kOutput, calls=%fused_computation.13 | convolution fusion | flops 6356992 | bytes 197664 | tf_op jit(solution)/shard_map/dot_general | solution.py:74
  (11 shorter events, 0.1 us)
Async XLA Ops:
  6.5 32.7 %copy-start = (bf16[1,352,2048]{2,1,0:T(8,128)(2,1)S(1)}, bf16[1,352,2048]{2,1,0:T(8,128)(2,1)}, u32[]{:S(2)}) copy-start(bf16[1,352,2048]{2,1,0:T(8,128)(2,1)} %param.17) | copy-start | bytes 4325380
  6.5 56.1 %reduce-scatter.5.cloned.1.call-start = ((), (), s32[]{:S(2)}) async-start(), calls=%async_computation.5 | async-start | bytes 655360 | tf_op jit(solution)/shard_map/reduce_scatter | solution.py:27
  20.6 1.3 %collective-permute-start = (bf16[4,8,2048]{2,1,0:T(8,128)(2,1)S(1)}, bf16[4,8,2048]{2,1,0:T(8,128)(2,1)S(1)}, u32[]{:S(2)}, u32[]{:S(2)}) collective-permute-start(bf16[4,8,2048]{2,1,0:T(8,128)(2,1)S(1)} %all_to_all.10), channel_id=1, source_target_pairs={{0,1},{1,0},{2,3},{3,2},{4,5},{5,4},{6,7},{7,6},{8,9},{9,8},{10,11... | collective-permute-start | bytes 393224 | tf_op jit(solution)/shard_map/ppermute | solution.py:11
  22.0 15.2 %collective-permute-start.1 = (bf16[8,8,2048]{2,1,0:T(8,128)(2,1)S(1)}, bf16[8,8,2048]{2,1,0:T(8,128)(2,1)S(1)}, u32[]{:S(2)}, u32[]{:S(2)}) collective-permute-start(bf16[8,8,2048]{2,1,0:T(8,128)(2,1)S(1)} %maximum_select_fusion.1), channel_id=1, source_target_pairs={{0,2},{1,3},{2,0},{3,1},{4,6},{5,7},{6,4},{7,5},{8,10},{9,11},{10,... | collective-permute-start | bytes 786440 | tf_op jit(solution)/shard_map/ppermute | solution.py:11
  42.6 41.7 %reduce-scatter.3.cloned.1.call-start = ((), (), s32[]{:S(2)}) async-start(), calls=%async_computation.4 | async-start | bytes 163840 | tf_op jit(solution)/shard_map/reduce_scatter | solution.py:81
  46.4 7.3 %copy-start.3 = (bf16[8,4]{0,1:T(4,128)(2,1)S(1)}, bf16[8,4]{0,1:T(4,128)(2,1)}, u32[]{:S(2)}) copy-start(bf16[8,4]{0,1:T(4,128)(2,1)} %param.12) | copy-start | bytes 196
  46.4 7.4 %copy-start.2 = (bf16[2048]{0:T(1024)(128)(2,1)S(1)}, bf16[2048]{0:T(1024)(128)(2,1)}, u32[]{:S(2)}) copy-start(bf16[2048]{0:T(1024)(128)(2,1)} %param.13) | copy-start | bytes 12292
  46.4 20.9 %copy-start.1 = (bf16[8,2048]{1,0:T(8,128)(2,1)S(1)}, bf16[8,2048]{1,0:T(8,128)(2,1)}, u32[]{:S(2)}) copy-start(bf16[8,2048]{1,0:T(8,128)(2,1)} %param.9) | copy-start | bytes 98308
  62.6 21.7 %all-to-all-start.1 = ((bf16[4,8,2048]{2,1,0:T(8,128)(2,1)}), bf16[4,8,2048]{2,1,0:T(8,128)(2,1)S(1)}, u32[]{:S(2)}, u32[]{:S(2)}) async-start(bf16[4,8,2048]{2,1,0:T(8,128)(2,1)} %reduce-scatter.5.cloned.1.call-done), calls=%async_computation.3 | async-start | bytes 262144 | tf_op jit(solution)/shard_map/all_to_all | solution.py:61
Sparse Core Ops, SparseCore 0:
  42.8 19.8 reduce-scatter.4
  64.9 19.4 reduce-scatter.2
